TPU v7x, 32 devices: a whole 2x2x4 slice. The times are simulated.
32 devices in a mesh: row: 8 (over y, x, core), col: 4 (over z).
Axes of the slice: x: 2, y: 2, z: 4, core: 2. Of those that a mesh axis runs over, the one named last changes fastest.
Arguments:
- signal: float32 [128, 128, 16, 256], P('row', 'col'), may hold values from -40 to 40, as said below
- start_frames: float32 [256, 32], replicated, may hold values from -6 to 6
- start_sends: float32 [16, 8], replicated, may hold values from -6 to 6
- start_rows: float32 [128, 64], replicated, may hold values from -6 to 6
- start_cols: float32 [128, 64], replicated, may hold values from -6 to 6
- rank_frames: int32 [1], replicated, may hold values from 16 to 32
- rank_sends: int32 [1], replicated, may hold values from 4 to 8
Outputs:
- filtered: float32 [128, 128, 16, 256], P('row', 'col')
Inputs may be any that keep to these rules, and one draw needn't show every extreme that they name: `signal`: beamformed samples.
All inputs are finite; a program needn't handle non-finite values.
Results may differ from a plain program's by a relative error of at most 0.0003.
Values sent between devices are 32-bit elements; how exact they have to be, the bound alone decides.
No kernel may reach another device: no remote copies, remote signals or barrier semaphores. Data moves between devices by JAX's collectives and lax.ppermute only.
A program may use at most 128 MiB of HBM per device.

v0:
```python
import jax
import jax.numpy as jnp
from jax import lax
from jax.sharding import PartitionSpec as P

NT = 256
NK = 16
TMAX = 32
KMAX = 8
RS = 64
ITERS = 2
CORE_W = 256


def orthonormal(gram, start):
    high = lax.Precision.HIGHEST
    basis = start
    for rounds in range(ITERS):
        image = jnp.dot(gram, basis, precision=high)
        inner = jnp.dot(image.T, image, precision=high)
        factor = jnp.linalg.cholesky(inner)
        basis = jax.scipy.linalg.solve_triangular(factor, image.T, lower=True).T
    return basis


def local(signal, start_frames, start_sends, start_rows, start_cols, rank_frames, rank_sends):
    high = lax.Precision.HIGHEST
    rows_dev, cols_dev = (signal.shape[0], signal.shape[1])
    pixels = rows_dev * cols_dev
    flattened = signal.reshape(-1, NT)
    blocks = signal.reshape(pixels, NK, NT)
    local_frames = jnp.einsum("pt,pu->tu", flattened, flattened, precision=high)
    local_sends = jnp.einsum("pkt,pjt->kj", blocks, blocks, precision=high)
    gram_frames, gram_sends = lax.psum((local_frames, local_sends), ("row", "col"))
    keep_frames = (jnp.arange(TMAX, dtype=jnp.int32) < rank_frames[0]).astype(jnp.float32)
    keep_sends = (jnp.arange(KMAX, dtype=jnp.int32) < rank_sends[0]).astype(jnp.float32)
    basis_frames = orthonormal(gram_frames, start_frames) * keep_frames[None, :]
    basis_sends = orthonormal(gram_sends, start_sends) * keep_sends[None, :]
    reduced = jnp.dot(flattened, basis_frames, precision=high).reshape(pixels, NK, TMAX)
    core = jnp.einsum("pkb,ka->pab", reduced, basis_sends, precision=high)
    core = core.reshape(rows_dev, cols_dev, CORE_W)
    gathered = lax.all_gather(core, "row", axis=0, tiled=True)
    total_rows = gathered.shape[0]
    unfolded = gathered.reshape(total_rows, -1)
    local_rows = jnp.dot(unfolded, unfolded.T, precision=high)
    gram_rows = lax.psum(local_rows, "col")
    basis_rows = orthonormal(gram_rows, start_rows)
    second = jnp.dot(basis_rows.T, unfolded, precision=high).reshape(RS, cols_dev, CORE_W)
    width = CORE_W // lax.axis_size("row")
    own_slice = lax.dynamic_slice_in_dim(second, lax.axis_index("row") * width, width, 2)
    across = lax.all_gather(own_slice, "col", axis=1, tiled=True)
    local_cols = jnp.einsum("sce,sde->cd", across, across, precision=high)
    gram_cols = lax.psum(local_cols, "row")
    basis_cols = orthonormal(gram_cols, start_cols)
    third_slice = jnp.einsum("cu,sce->sue", basis_cols, across, precision=high)
    third = lax.all_gather(third_slice, "row", axis=2, tiled=True)
    cols_own = lax.dynamic_slice_in_dim(basis_cols, lax.axis_index("col") * cols_dev, cols_dev, 0)
    rows_own = lax.dynamic_slice_in_dim(basis_rows, lax.axis_index("row") * rows_dev, rows_dev, 0)
    back_cols = jnp.einsum("cu,sue->sce", cols_own, third, precision=high)
    tissue_core = jnp.dot(rows_own, back_cols.reshape(RS, -1), precision=high)
    tissue_core = tissue_core.reshape(pixels, KMAX, TMAX)
    expanded = jnp.einsum("pab,ka->pkb", tissue_core, basis_sends, precision=high)
    tissue = jnp.dot(expanded.reshape(-1, TMAX), basis_frames.T, precision=high).reshape(
        signal.shape
    )
    return signal - tissue


def solution(mesh):
    return jax.shard_map(
        local,
        mesh=mesh,
        in_specs=(P("row", "col", None, None), P(), P(), P(), P(), P(), P()),
        out_specs=P("row", "col", None, None),
        check_vma=False,
    )
```

profile of v0, /device:TPU:0, one launch (start us, length us, event | category | flops | bytes accessed | tf_op | source)
XLA Modules:
  0.0 528.9 jit_solution(3371056779634263745)
XLA Ops:
  6.5 17.7 %convolution_bitcast_fusion.4 = f32[256,256]{1,0:T(8,128)} fusion(f32[16,32,16,256]{3,2,1,0:T(8,128)} %param.16), kind=kOutput, calls=%fused_computation.9 | convolution fusion | flops 6442450944 | bytes 8650752 | tf_op jit(solution)/shard_map/pt,pu->tu/dot_general | solution.py:32
  24.3 14.1 %convolution_bitcast_fusion.6 = f32[16,16]{1,0:T(8,128)S(1)} fusion(f32[16,32,16,256]{3,2,1,0:T(8,128)} %param.16), kind=kOutput, calls=%fused_computation.13 | convolution fusion | flops 402653184 | bytes 8389632 | tf_op jit(solution)/shard_map/pkt,pjt->kj/dot_general | solution.py:33
  39.8 42.4 %psum.28 = f32[16,16]{1,0:T(8,128)S(1)} all-reduce(f32[16,16]{1,0:T(8,128)S(1)} %convolution_bitcast_fusion.6), channel_id=1, replica_groups=mesh['row'=8,'col'=4] {'row','col'}, use_global_device_ids=true, to_apply=%region_0.0 | all-reduce | flops 256 | bytes 2048 | tf_op jit(solution)/shard_map/psum | solution.py:34
  88.6 65.3 %all-reduce.4.cloned.1.call-done = f32[256,256]{1,0:T(8,128)} async-done(((f32[256,256]{1,0:T(8,128)}), f32[256,256]{1,0:T(8,128)}) %all-reduce.4.cloned.1.call-update) | async-done | bytes 262160 | tf_op jit(solution)/shard_map/psum | solution.py:34
  170.9 9.9 %convolution_bitcast_fusion = f32[8192,32]{0,1:T(8,128)S(1)} fusion(f32[32,256]{1,0:T(8,128)S(1)} %convolution_multiply_fusion, f32[8192,256]{1,0:T(8,128)} %bitcast.199), kind=kOutput, calls=%fused_computation | convolution fusion | flops 805306368 | bytes 9469952 | tf_op jit(solution)/shard_map/dot_general | solution.py:39
  190.2 35.5 %all-gather.4.cloned.1.call-done = f32[128,32,256]{2,0,1:T(8,128)} async-done(((f32[16,32,256]{2,0,1:T(8,128)}), f32[128,32,256]{2,0,1:T(8,128)}) %all-gather.4.cloned.1.call-update) | async-done | bytes 4194320 | tf_op jit(solution)/shard_map/all_gather | solution.py:42
  225.7 7.6 %convolution_bitcast_fusion.5 = f32[128,128]{1,0:T(8,128)} fusion(f32[128,32,256]{2,0,1:T(8,128)} %all-gather.4.cloned.1.call-done), kind=kOutput, calls=%fused_computation.11 | convolution fusion | flops 1610612736 | bytes 4259840 | tf_op jit(solution)/shard_map/dot_general | solution.py:45
  233.4 5.6 %copy.60 = f32[128,32,256]{0,2,1:T(8,128)} copy(f32[128,32,256]{2,0,1:T(8,128)} %all-gather.4.cloned.1.call-done) | data formatting | bytes 8388608 | tf_op jit(solution)/shard_map/all_gather | solution.py:42
  239.0 28.8 %all-reduce.6.cloned.1.call-done = f32[128,128]{1,0:T(8,128)} async-done(((f32[128,128]{1,0:T(8,128)}), f32[128,128]{1,0:T(8,128)}) %all-reduce.6.cloned.1.call-update) | async-done | bytes 65552 | tf_op jit(solution)/shard_map/psum | solution.py:46
  269.2 5.8 %cholesky.202 = f32[64,64]{1,0:T(8,128)S(1)} custom-call(f32[64,64]{1,0:T(8,128)S(1)} %fusion.32), custom_call_target="Cholesky" | custom-call | tf_op jit(solution)/shard_map/jit(cholesky)/cholesky | solution.py:21
  276.5 4.9 custom-call.24
  283.0 5.8 %cholesky.213 = f32[64,64]{1,0:T(8,128)S(1)} custom-call(f32[64,64]{1,0:T(8,128)S(1)} %fusion.28), custom_call_target="Cholesky" | custom-call | tf_op jit(solution)/shard_map/jit(cholesky)/cholesky | solution.py:21
  290.3 4.9 custom-call.25
  295.5 5.4 %fusion = f32[64,32,256]{0,2,1:T(8,128)S(1)} fusion(f32[128,32,256]{0,2,1:T(8,128)} %copy.60, f32[64,128]{1,0:T(8,128)S(1)} %fusion.25), kind=kOutput, calls=%fused_computation.1 | convolution fusion | flops 805306368 | bytes 6324224 | tf_op jit(solution)/shard_map/dot_general | solution.py:48
  302.2 45.0 %all-gather.6.cloned.1.call-done = f32[64,128,32]{0,2,1:T(8,128)} async-done(((f32[64,32,32]{0,2,1:T(8,128)}), f32[64,128,32]{0,2,1:T(8,128)}) %all-gather.6.cloned.1.call-update) | async-done | bytes 1048592 | tf_op jit(solution)/shard_map/all_gather | solution.py:51
  347.2 7.0 %fusion.4 = f32[128,128]{1,0:T(8,128)} fusion(f32[64,128,32]{0,2,1:T(8,128)} %all-gather.6.cloned.1.call-done), kind=kOutput, calls=%fused_computation.10 | convolution fusion | flops 402653184 | bytes 1114112 | tf_op jit(solution)/shard_map/sce,sde->cd/dot_general | solution.py:52
  357.4 49.1 %all-reduce.8.cloned.1.call-done = f32[128,128]{1,0:T(8,128)} async-done(((f32[128,128]{1,0:T(8,128)}), f32[128,128]{1,0:T(8,128)}) %all-reduce.8.cloned.1.call-update) | async-done | bytes 65552 | tf_op jit(solution)/shard_map/psum | solution.py:53
  407.8 5.8 %cholesky.224 = f32[64,64]{1,0:T(8,128)S(1)} custom-call(f32[64,64]{1,0:T(8,128)S(1)} %fusion.23), custom_call_target="Cholesky" | custom-call | tf_op jit(solution)/shard_map/jit(cholesky)/cholesky | solution.py:21
  415.0 4.9 custom-call.26
  421.5 5.8 %cholesky.235 = f32[64,64]{1,0:T(8,128)S(1)} custom-call(f32[64,64]{1,0:T(8,128)S(1)} %fusion.19), custom_call_target="Cholesky" | custom-call | tf_op jit(solution)/shard_map/jit(cholesky)/cholesky | solution.py:21
  428.7 4.9 custom-call.27
  435.8 53.8 %all-gather.8.cloned.1.call-done = f32[64,64,256]{1,2,0:T(8,128)} async-done(((f32[64,64,32]{1,2,0:T(8,128)}), f32[64,64,256]{1,2,0:T(8,128)}) %all-gather.8.cloned.1.call-update) | async-done | bytes 4194320 | tf_op jit(solution)/shard_map/all_gather | solution.py:56
  489.6 11.5 %fusion.13 = f32[64,256,32]{1,2,0:T(8,128)S(1)} fusion(f32[64,64,256]{1,2,0:T(8,128)} %all-gather.8.cloned.1.call-done, f32[64,128]{1,0:T(8,128)S(1)} %fusion.16, s32[]{:T(128)S(6)} %select_n.20), kind=kOutput, calls=%fused_computation.25 | convolution fusion | flops 402653184 | bytes 6324228 | tf_op jit(solution)/shard_map/cu,sue->sce/dot_general | solution.py:59
  510.0 11.8 %convolution_subtract_fusion = f32[16,32,16,256]{3,2,1,0:T(8,128)} fusion(f32[16,32,16,256]{3,2,1,0:T(8,128)} %param.16, f32[16,32,16,32]{3,2,1,0:T(8,128)} %bitcast.200, f32[32,256]{1,0:T(8,128)S(1)} %convolution_multiply_fusion), kind=kOutput, calls=%fused_computation.3 | convolution fusion | flops 807403520 | bytes 17858560 | tf_op jit(solution)/shard_map/dot_general | solution.py:63
  (111 shorter events, 60.0 us)
Async XLA Ops:
  6.5 147.4 %copy-start = (f32[256,32]{0,1:T(8,128)S(1)}, f32[256,32]{0,1:T(8,128)}, u32[]{:S(2)}) copy-start(f32[256,32]{0,1:T(8,128)} %param.17) | copy-start | bytes 98308
  6.5 147.4 %all-reduce.4.cloned.1.call-start = ((), (), s32[]{:S(2)}) async-start(), calls=%async_computation | async-start | bytes 524288 | tf_op jit(solution)/shard_map/psum | solution.py:34
  24.3 57.9 %copy-start.4 = (f32[16,8]{0,1:T(8,128)S(1)}, f32[16,8]{0,1:T(8,128)}, u32[]{:S(2)}) copy-start(f32[16,8]{0,1:T(8,128)} %param.18) | copy-start | bytes 1540
  24.3 201.5 %all-gather.4.cloned.1.call-start = ((), (), s32[]{:S(2)}) async-start(), calls=%async_computation.1 | async-start | bytes 4718592 | tf_op jit(solution)/shard_map/all_gather | solution.py:42
  189.9 77.9 %all-reduce.6.cloned.1.call-start = ((), (), s32[]{:S(2)}) async-start(), calls=%async_computation.2 | async-start | bytes 131072 | tf_op jit(solution)/shard_map/psum | solution.py:46
  233.3 113.9 %all-gather.6.cloned.1.call-start = ((), (), s32[]{:S(2)}) async-start(), calls=%async_computation.3 | async-start | bytes 2621440 | tf_op jit(solution)/shard_map/all_gather | solution.py:51
  233.4 34.4 %copy-start.2 = (f32[128,64]{0,1:T(8,128)S(1)}, f32[128,64]{0,1:T(8,128)}, u32[]{:S(2)}) copy-start(f32[128,64]{0,1:T(8,128)} %param.19) | copy-start | bytes 98308
  300.9 105.6 %copy-start.3 = (f32[128,64]{0,1:T(8,128)S(1)}, f32[128,64]{0,1:T(8,128)}, u32[]{:S(2)}) copy-start(f32[128,64]{0,1:T(8,128)} %param.20) | copy-start | bytes 98308
  301.7 104.7 %all-reduce.8.cloned.1.call-start = ((), (), s32[]{:S(2)}) async-start(), calls=%async_computation.4 | async-start | bytes 131072 | tf_op jit(solution)/shard_map/psum | solution.py:53
  354.3 135.3 %all-gather.8.cloned.1.call-start = ((), (), s32[]{:S(2)}) async-start(), calls=%async_computation.5 | async-start | bytes 9437184 | tf_op jit(solution)/shard_map/all_gather | solution.py:56
  510.0 11.8 %copy-start.1 = (f32[256,32]{0,1:T(8,128)S(1)}, f32[256,32]{0,1:T(8,128)}, u32[]{:S(2)}) copy-start(f32[256,32]{0,1:T(8,128)} %param.17) | copy-start | bytes 98308
Sparse Core Ops, SparseCore 0:
  24.4 129.5 all-reduce.3
  190.1 35.6 all-gather.3
  233.5 34.2 all-reduce.5
  301.9 45.3 all-gather.5
  354.4 51.9 all-reduce.7
  435.9 53.6 all-gather.7
where the time goes:
time: 537 us; the launch traced here: 529 us
  waiting for transfers between devices  278 us (52%)
  matrix products  100 us (19%)
  other arithmetic  67.3 us (13%)
  blocking collectives  42.4 us (8%)
  local copies, waits for them, and re-layouts  25.1 us (5%)
  between operations  15.5 us (3%)
    psum x1, waiting for transfers between devices, local(): lax.psum((local_frames, local_sends), ('row', 'col'))  65.3 us
    all_gather x1, waiting for transfers between devices, local(): third = lax.all_gather(third_slice, 'row', axis=2, tiled=True)  53.8 us
    psum x1, waiting for transfers between devices, local(): gram_cols = lax.psum(local_cols, 'row')  49.1 us
    all_gather x1, waiting for transfers between devices, local(): across = lax.all_gather(own_slice, 'col', axis=1, tiled=True)  45 us
    psum x1, blocking collectives, local(): lax.psum((local_frames, local_sends), ('row', 'col'))  42.4 us
    another operation x24, other arithmetic, orthonormal(): factor = jnp.linalg.cholesky(inner)  36.3 us
    all_gather x1, waiting for transfers between devices, local(): gathered = lax.all_gather(core, 'row', axis=0, tiled=True)  35.5 us
    another operation x16, other arithmetic, orthonormal(): basis = jax.scipy.linalg.solve_triangular(factor, image.T, lower=True).T  31 us
  transfers between devices with their start and end apart: 6, of which 6 were waited for; matrix products, arithmetic and copies ran while one was open for 6% of the time, Pallas kernels for 0%

commit v1 on v0

--- a/solution.py
+++ b/solution.py
@@ -50,7 +50,11 @@
     own_slice = lax.dynamic_slice_in_dim(second, lax.axis_index("row") * width, width, 2)
     across = lax.all_gather(own_slice, "col", axis=1, tiled=True)
     local_cols = jnp.einsum("sce,sde->cd", across, across, precision=high)
-    gram_cols = lax.psum(local_cols, "row")
+    gram_cols = local_cols
+    for hop in (1, 2, 4):
+        gram_cols = gram_cols + lax.ppermute(
+            gram_cols, "row", [(dev, dev ^ hop) for dev in range(8)]
+        )
     basis_cols = orthonormal(gram_cols, start_cols)
     third_slice = jnp.einsum("cu,sce->sue", basis_cols, across, precision=high)
     third = lax.all_gather(third_slice, "row", axis=2, tiled=True)

time: 537 us -> 492 us (0.916)
  waiting for transfers between devices: 278 us -> 232 us
    psum x1 -> x0, waiting for transfers between devices: 49.1 us -> none  [local(): gram_cols = lax.psum(local_cols, 'row')]
  transfers between devices with their start and end apart: 6 -> 8, of which waited for: 6 -> 7; matrix products, arithmetic and copies ran while one was open for 6% -> 6% of each run, Pallas kernels for 0% -> 0%
where the time goes in v1:
time: 492 us; the launch traced here: 484 us
  waiting for transfers between devices  232 us (47%)
  matrix products  97.8 us (20%)
  other arithmetic  67.4 us (14%)
  blocking collectives  42.4 us (9%)
  local copies, waits for them, and re-layouts  25.1 us (5%)
  between operations  15.2 us (3%)
    psum x1, waiting for transfers between devices, local(): lax.psum((local_frames, local_sends), ('row', 'col'))  65.3 us
    all_gather x1, waiting for transfers between devices, local(): third = lax.all_gather(third_slice, 'row', axis=2, tiled=True)  53 us
    all_gather x1, waiting for transfers between devices, local(): across = lax.all_gather(own_slice, 'col', axis=1, tiled=True)  45 us
    psum x1, blocking collectives, local(): lax.psum((local_frames, local_sends), ('row', 'col'))  42.4 us
    another operation x24, other arithmetic, orthonormal(): factor = jnp.linalg.cholesky(inner)  36.3 us
    all_gather x1, waiting for transfers between devices, local(): gathered = lax.all_gather(core, 'row', axis=0, tiled=True)  35.5 us
    another operation x16, other arithmetic, orthonormal(): basis = jax.scipy.linalg.solve_triangular(factor, image.T, lower=True).T  31 us
    psum x1, waiting for transfers between devices, local(): gram_rows = lax.psum(local_rows, 'col')  28.8 us
  transfers between devices with their start and end apart: 8, of which 7 were waited for; matrix products, arithmetic and copies ran while one was open for 6% of the time, Pallas kernels for 0%

profile of v1, /device:TPU:0, one launch (start us, length us, event | category | flops | bytes accessed | tf_op | source)
XLA Modules:
  0.0 483.6 jit_solution(12612667114300696734)
XLA Ops:
  6.5 17.7 %convolution_bitcast_fusion.4 = f32[256,256]{1,0:T(8,128)} fusion(f32[16,32,16,256]{3,2,1,0:T(8,128)} %param.16), kind=kOutput, calls=%fused_computation.9 | convolution fusion | flops 6442450944 | bytes 8650752 | tf_op jit(solution)/shard_map/pt,pu->tu/dot_general | solution.py:32
  24.3 14.1 %convolution_bitcast_fusion.6 = f32[16,16]{1,0:T(8,128)S(1)} fusion(f32[16,32,16,256]{3,2,1,0:T(8,128)} %param.16), kind=kOutput, calls=%fused_computation.13 | convolution fusion | flops 402653184 | bytes 8389632 | tf_op jit(solution)/shard_map/pkt,pjt->kj/dot_general | solution.py:33
  39.8 42.4 %psum.21 = f32[16,16]{1,0:T(8,128)S(1)} all-reduce(f32[16,16]{1,0:T(8,128)S(1)} %convolution_bitcast_fusion.6), channel_id=1, replica_groups=mesh['row'=8,'col'=4] {'row','col'}, use_global_device_ids=true, to_apply=%region_0.0 | all-reduce | flops 256 | bytes 2048 | tf_op jit(solution)/shard_map/psum | solution.py:34
  88.6 65.3 %all-reduce.3.cloned.1.call-done = f32[256,256]{1,0:T(8,128)} async-done(((f32[256,256]{1,0:T(8,128)}), f32[256,256]{1,0:T(8,128)}) %all-reduce.3.cloned.1.call-update) | async-done | bytes 262160 | tf_op jit(solution)/shard_map/psum | solution.py:34
  170.9 9.9 %convolution_bitcast_fusion = f32[8192,32]{0,1:T(8,128)S(1)} fusion(f32[32,256]{1,0:T(8,128)S(1)} %convolution_multiply_fusion, f32[8192,256]{1,0:T(8,128)} %bitcast.199), kind=kOutput, calls=%fused_computation | convolution fusion | flops 805306368 | bytes 9469952 | tf_op jit(solution)/shard_map/dot_general | solution.py:39
  190.2 35.5 %all-gather.4.cloned.1.call-done = f32[128,32,256]{2,0,1:T(8,128)} async-done(((f32[16,32,256]{2,0,1:T(8,128)}), f32[128,32,256]{2,0,1:T(8,128)}) %all-gather.4.cloned.1.call-update) | async-done | bytes 4194320 | tf_op jit(solution)/shard_map/all_gather | solution.py:42
  225.7 7.6 %convolution_bitcast_fusion.5 = f32[128,128]{1,0:T(8,128)} fusion(f32[128,32,256]{2,0,1:T(8,128)} %all-gather.4.cloned.1.call-done), kind=kOutput, calls=%fused_computation.11 | convolution fusion | flops 1610612736 | bytes 4259840 | tf_op jit(solution)/shard_map/dot_general | solution.py:45
  233.4 5.6 %copy.60 = f32[128,32,256]{0,2,1:T(8,128)} copy(f32[128,32,256]{2,0,1:T(8,128)} %all-gather.4.cloned.1.call-done) | data formatting | bytes 8388608 | tf_op jit(solution)/shard_map/all_gather | solution.py:42
  239.0 28.8 %all-reduce.5.cloned.1.call-done = f32[128,128]{1,0:T(8,128)} async-done(((f32[128,128]{1,0:T(8,128)}), f32[128,128]{1,0:T(8,128)}) %all-reduce.5.cloned.1.call-update) | async-done | bytes 65552 | tf_op jit(solution)/shard_map/psum | solution.py:46
  269.2 5.8 %cholesky.202 = f32[64,64]{1,0:T(8,128)S(1)} custom-call(f32[64,64]{1,0:T(8,128)S(1)} %fusion.32), custom_call_target="Cholesky" | custom-call | tf_op jit(solution)/shard_map/jit(cholesky)/cholesky | solution.py:21
  276.5 4.9 %custom-call.24 = f32[1,64,64]{1,2,0:T(8,128)S(1)} custom-call(f32[1,64,64]{2,1,0:T(8,128)S(1)} %fusion.8), custom_call_target="InvertDiagBlocksLowerTriangular" | custom-call | tf_op jit(solution)/shard_map/jit(_solve_triangular)/triangular_solve | solution.py:22
  283.0 5.8 %cholesky.213 = f32[64,64]{1,0:T(8,128)S(1)} custom-call(f32[64,64]{1,0:T(8,128)S(1)} %fusion.28), custom_call_target="Cholesky" | custom-call | tf_op jit(solution)/shard_map/jit(cholesky)/cholesky | solution.py:21
  290.3 4.9 %custom-call.25 = f32[1,64,64]{1,2,0:T(8,128)S(1)} custom-call(f32[1,64,64]{2,1,0:T(8,128)S(1)} %fusion.9), custom_call_target="InvertDiagBlocksLowerTriangular" | custom-call | tf_op jit(solution)/shard_map/jit(_solve_triangular)/triangular_solve | solution.py:22
  295.5 5.4 %fusion = f32[64,32,256]{0,2,1:T(8,128)S(1)} fusion(f32[128,32,256]{0,2,1:T(8,128)} %copy.60, f32[64,128]{1,0:T(8,128)S(1)} %fusion.25), kind=kOutput, calls=%fused_computation.1 | convolution fusion | flops 805306368 | bytes 6324224 | tf_op jit(solution)/shard_map/dot_general | solution.py:48
  302.2 45.0 %all-gather.6.cloned.1.call-done = f32[64,128,32]{0,2,1:T(8,128)} async-done(((f32[64,32,32]{0,2,1:T(8,128)}), f32[64,128,32]{0,2,1:T(8,128)}) %all-gather.6.cloned.1.call-update) | async-done | bytes 1048592 | tf_op jit(solution)/shard_map/all_gather | solution.py:51
  347.2 6.4 %fusion.4 = f32[128,128]{1,0:T(8,128)S(1)} fusion(f32[64,128,32]{0,2,1:T(8,128)} %all-gather.6.cloned.1.call-done), kind=kOutput, calls=%fused_computation.10 | convolution fusion | flops 402653184 | bytes 1114112 | tf_op jit(solution)/shard_map/sce,sde->cd/dot_general | solution.py:52
  364.4 5.8 %cholesky.224 = f32[64,64]{1,0:T(8,128)S(1)} custom-call(f32[64,64]{1,0:T(8,128)S(1)} %fusion.23), custom_call_target="Cholesky" | custom-call | tf_op jit(solution)/shard_map/jit(cholesky)/cholesky | solution.py:21
  371.6 4.9 %custom-call.26 = f32[1,64,64]{1,2,0:T(8,128)S(1)} custom-call(f32[1,64,64]{2,1,0:T(8,128)S(1)} %fusion.10), custom_call_target="InvertDiagBlocksLowerTriangular" | custom-call | tf_op jit(solution)/shard_map/jit(_solve_triangular)/triangular_solve | solution.py:22
  377.3 5.8 %cholesky.235 = f32[64,64]{1,0:T(8,128)S(1)} custom-call(f32[64,64]{1,0:T(8,128)S(1)} %fusion.19), custom_call_target="Cholesky" | custom-call | tf_op jit(solution)/shard_map/jit(cholesky)/cholesky | solution.py:21
  384.5 4.9 %custom-call.27 = f32[1,64,64]{1,2,0:T(8,128)S(1)} custom-call(f32[1,64,64]{2,1,0:T(8,128)S(1)} %fusion.11), custom_call_target="InvertDiagBlocksLowerTriangular" | custom-call | tf_op jit(solution)/shard_map/jit(_solve_triangular)/triangular_solve | solution.py:22
  391.6 53.0 %all-gather.8.cloned.1.call-done = f32[64,64,256]{1,2,0:T(8,128)} async-done(((f32[64,64,32]{1,2,0:T(8,128)}), f32[64,64,256]{1,2,0:T(8,128)}) %all-gather.8.cloned.1.call-update) | async-done | bytes 4194320 | tf_op jit(solution)/shard_map/all_gather | solution.py:60
  444.6 11.5 %fusion.13 = f32[64,256,32]{1,2,0:T(8,128)S(1)} fusion(f32[64,64,256]{1,2,0:T(8,128)} %all-gather.8.cloned.1.call-done, f32[64,128]{1,0:T(8,128)S(1)} %fusion.16, s32[]{:T(128)S(6)} %select_n.20), kind=kOutput, calls=%fused_computation.25 | convolution fusion | flops 402653184 | bytes 6324228 | tf_op jit(solution)/shard_map/cu,sue->sce/dot_general | solution.py:63
  461.1 3.8 copy.74
  464.9 11.8 %convolution_subtract_fusion = f32[16,32,16,256]{3,2,1,0:T(8,128)} fusion(f32[16,32,16,256]{3,2,1,0:T(8,128)} %param.16, f32[16,32,16,32]{3,2,1,0:T(8,128)} %bitcast.200, f32[32,256]{1,0:T(8,128)S(1)} %convolution_multiply_fusion), kind=kOutput, calls=%fused_computation.3 | convolution fusion | flops 807403520 | bytes 17858560 | tf_op jit(solution)/shard_map/dot_general | solution.py:67
  (117 shorter events, 61.6 us)
Async XLA Ops:
  6.5 147.4 %copy-start = (f32[256,32]{0,1:T(8,128)S(1)}, f32[256,32]{0,1:T(8,128)}, u32[]{:S(2)}) copy-start(f32[256,32]{0,1:T(8,128)} %param.17) | copy-start | bytes 98308
  6.5 147.4 %all-reduce.3.cloned.1.call-start = ((), (), s32[]{:S(2)}) async-start(), calls=%async_computation | async-start | bytes 524288 | tf_op jit(solution)/shard_map/psum | solution.py:34
  24.3 57.9 %copy-start.4 = (f32[16,8]{0,1:T(8,128)S(1)}, f32[16,8]{0,1:T(8,128)}, u32[]{:S(2)}) copy-start(f32[16,8]{0,1:T(8,128)} %param.18) | copy-start | bytes 1540
  24.3 201.5 %all-gather.4.cloned.1.call-start = ((), (), s32[]{:S(2)}) async-start(), calls=%async_computation.1 | async-start | bytes 4718592 | tf_op jit(solution)/shard_map/all_gather | solution.py:42
  189.9 77.9 %all-reduce.5.cloned.1.call-start = ((), (), s32[]{:S(2)}) async-start(), calls=%async_computation.2 | async-start | bytes 131072 | tf_op jit(solution)/shard_map/psum | solution.py:46
  233.3 113.9 %all-gather.6.cloned.1.call-start = ((), (), s32[]{:S(2)}) async-start(), calls=%async_computation.3 | async-start | bytes 2621440 | tf_op jit(solution)/shard_map/all_gather | solution.py:51
  233.4 34.4 %copy-start.2 = (f32[128,64]{0,1:T(8,128)S(1)}, f32[128,64]{0,1:T(8,128)}, u32[]{:S(2)}) copy-start(f32[128,64]{0,1:T(8,128)} %param.19) | copy-start | bytes 98308
  300.9 63.0 %copy-start.3 = (f32[128,64]{0,1:T(8,128)S(1)}, f32[128,64]{0,1:T(8,128)}, u32[]{:S(2)}) copy-start(f32[128,64]{0,1:T(8,128)} %param.20) | copy-start | bytes 98308
  301.7 142.9 %all-gather.8.cloned.1.call-start = ((), (), s32[]{:S(2)}) async-start(), calls=%async_computation.4 | async-start | bytes 9437184 | tf_op jit(solution)/shard_map/all_gather | solution.py:60
  353.6 1.3 collective-permute-start
  355.0 4.3 collective-permute-start.1
  359.3 4.6 collective-permute-start.2
  464.9 11.8 %copy-start.1 = (f32[256,32]{0,1:T(8,128)S(1)}, f32[256,32]{0,1:T(8,128)}, u32[]{:S(2)}) copy-start(f32[256,32]{0,1:T(8,128)} %param.17) | copy-start | bytes 98308
Sparse Core Ops, SparseCore 0:
  24.4 129.5 all-reduce.2
  190.1 35.6 all-gather.3
  233.5 34.2 all-reduce.4
  301.9 45.3 all-gather.5
  391.7 52.8 all-gather.7
